TPU v7x, 256 devices: a 4x2x16 block of a 4x16x16 slice. The times are simulated.
256 devices in a mesh: frag: 2 (over y), gx: 128 (over x, z, core).
Axes of the slice: x: 4, y: 2, z: 16, core: 2. Of those that a mesh axis runs over, the one named last changes fastest.
The devices are a block of a 4x16x16 slice.
Arguments:
- coefficient: float32 [131072], P(('frag', 'gx')), parts along dimension 0, may hold values from 0.05 to 0.3
- exponent: float32 [131072], P(('frag', 'gx')), parts along dimension 0, may hold values from 0.05 to 0.5
- centers: float32 [3, 131072], P(None, ('frag', 'gx')), parts along dimension 1, may hold values from -2 to 2
- density: float32 [131072], P(('frag', 'gx')), parts along dimension 0, may hold values from -6 to 6
- core_fock: float32 [131072], P(('frag', 'gx')), parts along dimension 0, may hold values from -6 to 6
- shell_ang: int32 [512], P('frag'), parts along dimension 0, may hold values from 0 to 3, as said below
- tile_list: int32 [2, 32768], P(None, ('frag', 'gx')), parts along dimension 1, may hold values from 0 to 255, as said below
Outputs:
- fock: float32 [131072], P(('frag', 'gx')), parts along dimension 0
There are 2 independent parts, one for each index of `frag`. A program takes and returns all parts, laid end to end along the dimension named above; each array names one. Nothing has to cross between parts.
Inputs may be any that keep to these rules, and one draw needn't show every extreme that they name: `shell_ang`: each of 0 to 3 is the angular momentum of exactly 64 blocks; blocks 0 to 1 all have 0. `tile_list`: kind never falls along the list, and kinds 0 to 6 fill 1, 2, 3, 4, 3, 2, 1 sixteenths of the list in turn; pair block b is owned by index b // 2 of gx; among the 128 tiles of one index of gx at most 4 have bra blocks of one owner, and index 0 of gx holds exactly 4 tiles for owner 0.
All inputs are finite; a program needn't handle non-finite values.
Results may differ from a plain program's by a relative error of at most 0.0003.
Values sent between devices are 32-bit elements; how exact they have to be, the bound alone decides.
A program may use at most 128 MiB of HBM per device.

v0:
```python
import jax
import jax.numpy as jnp
from jax import lax
from jax.sharding import Mesh
from jax.sharding import PartitionSpec as P

PB = 256
MAXL = 3
TB = 32
GX = ("gx_0", "gx_1", "gx_2")
FRAG_GX = ("frag", "gx_0", "gx_1", "gx_2")


def laid_out(blocks, dim):
    blocks = jnp.moveaxis(blocks, 0, dim)
    shape = blocks.shape
    return blocks.reshape(*shape[:dim], shape[dim] * shape[dim + 1], *shape[dim + 2 :])


def gather_packed(arrays, axis, dims):
    vector = jnp.concatenate([a.reshape(-1) for a in arrays])
    lines, at, outs = (lax.all_gather(vector, axis), 0, [])
    for a, dim in zip(arrays, dims):
        blocks = lines[:, at : at + a.size].reshape(-1, *a.shape)
        outs.append(laid_out(blocks, dim))
        at += a.size
    return tuple(outs)


def in_blocks(x, dim, count):
    shape = x.shape
    blocks = x.reshape(*shape[:dim], count, shape[dim] // count, *shape[dim + 1 :])
    return jnp.moveaxis(blocks, dim, 0)


def edges_of(length, count):
    unit = 8 if length >= 8 * count else 1
    return [length // unit * k // count * unit for k in range(1, count)]


def sum_in_order(blocks, axes, order):
    shape = [lax.axis_size(a) for a in axes]
    blocks = blocks.reshape(*shape, *blocks.shape[1:])
    blocks = blocks.transpose(*order, *range(len(axes), blocks.ndim))
    blocks = blocks.reshape(-1, *blocks.shape[len(axes) :])
    for k in order:
        blocks = lax.psum_scatter(blocks, axes[k], scatter_dimension=0, tiled=True)
    return blocks[0]


def sum_at_once(x, axes, dim):
    blocks = in_blocks(x, dim, lax.axis_size(axes))
    split_at = max(range(1, max(2, blocks.ndim - 1)), key=lambda d: blocks.shape[d])
    count, outs = (len(axes), [])
    for leading, slab in enumerate(
        jnp.split(blocks, edges_of(blocks.shape[split_at], count), axis=split_at)
    ):
        if slab.size:
            order = [(leading + k) % count for k in range(count)]
            outs.append(sum_in_order(slab, axes, order))
    return jnp.concatenate(outs, axis=split_at - 1)


def tile_terms(tables, bra_ids, ket_ids, angular):
    exp_blocks, cen_blocks, coef_blocks, weight_blocks = tables
    bra_exp = exp_blocks[bra_ids]
    ket_exp = exp_blocks[ket_ids]
    bra_cen = cen_blocks[:, bra_ids]
    ket_cen = cen_blocks[:, ket_ids]
    distance = jnp.zeros((bra_exp.shape[0], bra_exp.shape[1], ket_exp.shape[1]), jnp.float32)
    for coordinate in range(3):
        offset = bra_cen[coordinate][:, :, None] - ket_cen[coordinate][:, None, :]
        distance = distance + offset * offset
    denominator = bra_exp[:, :, None] + ket_exp[:, None, :] + distance
    ratio = distance / denominator
    highest = jnp.max(angular)
    series_term = jnp.ones_like(ratio)
    series_sum = jnp.ones_like(ratio)
    for power in range(1, 2 * MAXL + 1):

        def add_power(carry, power=power):
            term_now, sum_now = carry
            term_now = term_now * ratio
            sum_now = sum_now + jnp.where(
                power <= angular[:, None, None], term_now / float(2 * power + 1), 0.0
            )
            return (term_now, sum_now)

        def keep_power(carry):
            return carry

        series_term, series_sum = lax.cond(
            power <= highest, add_power, keep_power, (series_term, series_sum)
        )
    kernel = series_sum * lax.rsqrt(denominator)
    kernel = kernel * coef_blocks[bra_ids][:, :, None] * coef_blocks[ket_ids][:, None, :]
    return jnp.einsum("tij,tj->ti", kernel, weight_blocks[ket_ids], precision=lax.Precision.HIGHEST)


def shards(coefficient, exponent, centers, density, core_fock, shell_ang, tile_list):
    devices = lax.axis_size(GX)
    local_tiles = tile_list.shape[1]
    exp_all, cen_all, coef_all, weight_all = gather_packed(
        (exponent, centers, coefficient, density), GX, (0, 1, 0, 0)
    )
    blocks_total = exp_all.shape[0] // PB
    tables = (
        exp_all.reshape(blocks_total, PB),
        cen_all.reshape(3, blocks_total, PB),
        coef_all.reshape(blocks_total, PB),
        weight_all.reshape(blocks_total, PB),
    )
    spread = tile_list.reshape(2, local_tiles // devices, devices)
    arrived = lax.all_to_all(spread, GX, split_axis=2, concat_axis=1, tiled=True)
    shuffled_tiles = arrived.reshape(2, local_tiles)
    kinds_raw = shell_ang[shuffled_tiles[0]] + shell_ang[shuffled_tiles[1]]
    ordering = jnp.argsort(kinds_raw, stable=True)
    listing = shuffled_tiles[:, ordering]
    angular = kinds_raw[ordering]
    row_ids = listing[0]
    presence = jnp.ones((listing.shape[1],), jnp.float32)
    rounds = listing.shape[1] // TB
    slots_total = listing.shape[1]
    tile_blocks = listing.reshape(2, slots_total // TB, TB)
    kind_blocks = angular.reshape(slots_total // TB, TB)
    row_blocks = row_ids.reshape(slots_total // TB, TB)
    presence_blocks = presence.reshape(slots_total // TB, TB)

    def add_block(position, coulomb):
        partial_value = tile_terms(
            tables, tile_blocks[0, position], tile_blocks[1, position], kind_blocks[position]
        )
        return coulomb.at[row_blocks[position]].add(
            partial_value * presence_blocks[position][:, None]
        )

    coulomb = lax.fori_loop(0, rounds, add_block, jnp.zeros((blocks_total, PB), jnp.float32))
    shares = sum_at_once(coulomb.reshape(blocks_total * PB), GX, 0)
    return core_fock + shares


def solution(mesh):
    finer = Mesh(
        mesh.devices.reshape(mesh.shape["frag"], 4, 16, 2), ("frag", "gx_0", "gx_1", "gx_2")
    )
    return jax.shard_map(
        shards,
        mesh=finer,
        in_specs=(
            P(FRAG_GX),
            P(FRAG_GX),
            P(None, FRAG_GX),
            P(FRAG_GX),
            P(FRAG_GX),
            P("frag"),
            P(None, FRAG_GX),
        ),
        out_specs=P(FRAG_GX),
        check_vma=False,
    )
```

profile of v0, /device:TPU:47, one launch (start us, length us, event | category | flops | bytes accessed | tf_op | source)
XLA Modules:
  0.0 666.7 jit_solution(5097625459969688022)
XLA Ops:
  10.1 31.4 %all-to-all-start = ((s32[2,1,128]{0,1,2:T(1,128)}), s32[2,1,128]{0,1,2:T(1,128)S(1)}, u32[]{:S(2)}, u32[]{:S(2)}) async-start(s32[2,1,128]{0,1,2:T(1,128)} %bitcast.15), calls=%async_computation | async-start | bytes 131072 | tf_op jit(solution)/shard_map/all_to_all | solution.py:114
  64.6 94.6 %all-gather.3.cloned.1.call-done = f32[393216]{0:T(1024)} async-done(((f32[3072]{0:T(1024)}), f32[393216]{0:T(1024)}) %all-gather.3.cloned.1.call-update) | async-done | bytes 1572880 | tf_op jit(solution)/shard_map/all_gather | solution.py:22
  162.3 341.1 %while.13 = (s32[]{:T(128)}, f32[256,256]{1,0:T(8,128)S(1)}, s32[4,32]{1,0:T(4,128)S(1)}, s32[4,32]{1,0:T(4,128)S(1)}, s32[2,4,32]{2,1,0:T(4,128)S(1)}, /*index=...) while((s32[]{:T(128)}, f32[256,256]{1,0:T(8,128)S(1)}, ...), condition=%wide.region_16.17_spmd, body=%wide.region_1.16_spmd.sunk | while | flops 123742736 | bytes 287682368 | solution.py:137
  186.1 15.6 %conditional.13 = ((f32[32,256,256]{2,1,0:T(8,128)}, f32[32,256,256]{2,1,0:T(8,128)})) conditional(s32[]{:T(128)} %convert_element_type.52, (f32[32,256,256]{2,1,0:T(8,128)}, f32[32,256,256]{2,1,0:T(8,128)}) %conditional.12, (f32[32,256,256]{2,1,0:T(8,128)}, f32[32,256,256]{2,1,0:T(8,128)}, s32[1,32]{1,0:T(1,128)S(1)}, ...), branch_computations={%region_5.5_spmd, %region_6.6_spmd} | conditional | flops 8388640 | bytes 41943256 | solution.py:92
  186.1 15.6 %select_add_fusion.1 = (f32[32,256,256]{2,1,0:T(8,128)}, f32[32,256,256]{2,1,0:T(8,128)}) fusion(f32[32,256,256]{2,1,0:T(8,128)} %get-tuple-element.223, pred[32]{0:T(512)(128)(4,1)S(1)} %compare_bitcast_fusion.1, f32[32,256,256]{2,1,0:T(8,128)} %get-tuple-element.221, f32[32,256,256]{2,1,0:T(8,128)} %get-tuple-element.222), kind=kLoop, calls=%fused_computation.14 | loop fusion | flops 8388608 | bytes 41943072 | tf_op jit(solution)/shard_map/while/body/eval_jaxpr/cond/branch_1_fun/add | solution.py:84
  244.7 15.6 %conditional.13 = ((f32[32,256,256]{2,1,0:T(8,128)}, f32[32,256,256]{2,1,0:T(8,128)})) conditional(s32[]{:T(128)} %convert_element_type.52, (f32[32,256,256]{2,1,0:T(8,128)}, f32[32,256,256]{2,1,0:T(8,128)}) %conditional.12, (f32[32,256,256]{2,1,0:T(8,128)}, f32[32,256,256]{2,1,0:T(8,128)}, s32[1,32]{1,0:T(1,128)S(1)}, ...), branch_computations={%region_5.5_spmd, %region_6.6_spmd} | conditional | flops 8388640 | bytes 41943256 | solution.py:92
  244.7 15.6 %select_add_fusion.1 = (f32[32,256,256]{2,1,0:T(8,128)}, f32[32,256,256]{2,1,0:T(8,128)}) fusion(f32[32,256,256]{2,1,0:T(8,128)} %get-tuple-element.223, pred[32]{0:T(512)(128)(4,1)S(1)} %compare_bitcast_fusion.1, f32[32,256,256]{2,1,0:T(8,128)} %get-tuple-element.221, f32[32,256,256]{2,1,0:T(8,128)} %get-tuple-element.222), kind=kLoop, calls=%fused_computation.14 | loop fusion | flops 8388608 | bytes 41943072 | tf_op jit(solution)/shard_map/while/body/eval_jaxpr/cond/branch_1_fun/add | solution.py:84
  260.9 15.6 %conditional.14 = ((f32[32,256,256]{2,1,0:T(8,128)}, f32[32,256,256]{2,1,0:T(8,128)})) conditional(s32[]{:T(128)} %convert_element_type.51, (f32[32,256,256]{2,1,0:T(8,128)}, f32[32,256,256]{2,1,0:T(8,128)}) %get-tuple-element.526, (f32[32,256,256]{2,1,0:T(8,128)}, f32[32,256,256]{2,1,0:T(8,128)}, s32[1,32]{1,0:T(1,128)S(1)}, ...), branch_computations={%region_7.7_spmd, %region_8.8_spmd} | conditional | flops 8388640 | bytes 41943256 | solution.py:92
  260.9 15.6 %select_add_fusion.2 = (f32[32,256,256]{2,1,0:T(8,128)}, f32[32,256,256]{2,1,0:T(8,128)}) fusion(f32[32,256,256]{2,1,0:T(8,128)} %get-tuple-element.227, pred[32]{0:T(512)(128)(4,1)S(1)} %compare_bitcast_fusion.2, f32[32,256,256]{2,1,0:T(8,128)} %get-tuple-element.225, f32[32,256,256]{2,1,0:T(8,128)} %get-tuple-element.226), kind=kLoop, calls=%fused_computation.16 | loop fusion | flops 8388608 | bytes 41943072 | tf_op jit(solution)/shard_map/while/body/eval_jaxpr/cond/branch_1_fun/add | solution.py:84
  318.9 15.6 %conditional.13 = ((f32[32,256,256]{2,1,0:T(8,128)}, f32[32,256,256]{2,1,0:T(8,128)})) conditional(s32[]{:T(128)} %convert_element_type.52, (f32[32,256,256]{2,1,0:T(8,128)}, f32[32,256,256]{2,1,0:T(8,128)}) %conditional.12, (f32[32,256,256]{2,1,0:T(8,128)}, f32[32,256,256]{2,1,0:T(8,128)}, s32[1,32]{1,0:T(1,128)S(1)}, ...), branch_computations={%region_5.5_spmd, %region_6.6_spmd} | conditional | flops 8388640 | bytes 41943256 | solution.py:92
  318.9 15.6 %select_add_fusion.1 = (f32[32,256,256]{2,1,0:T(8,128)}, f32[32,256,256]{2,1,0:T(8,128)}) fusion(f32[32,256,256]{2,1,0:T(8,128)} %get-tuple-element.223, pred[32]{0:T(512)(128)(4,1)S(1)} %compare_bitcast_fusion.1, f32[32,256,256]{2,1,0:T(8,128)} %get-tuple-element.221, f32[32,256,256]{2,1,0:T(8,128)} %get-tuple-element.222), kind=kLoop, calls=%fused_computation.14 | loop fusion | flops 8388608 | bytes 41943072 | tf_op jit(solution)/shard_map/while/body/eval_jaxpr/cond/branch_1_fun/add | solution.py:84
  335.1 15.6 %conditional.14 = ((f32[32,256,256]{2,1,0:T(8,128)}, f32[32,256,256]{2,1,0:T(8,128)})) conditional(s32[]{:T(128)} %convert_element_type.51, (f32[32,256,256]{2,1,0:T(8,128)}, f32[32,256,256]{2,1,0:T(8,128)}) %get-tuple-element.526, (f32[32,256,256]{2,1,0:T(8,128)}, f32[32,256,256]{2,1,0:T(8,128)}, s32[1,32]{1,0:T(1,128)S(1)}, ...), branch_computations={%region_7.7_spmd, %region_8.8_spmd} | conditional | flops 8388640 | bytes 41943256 | solution.py:92
  335.2 15.6 %select_add_fusion.2 = (f32[32,256,256]{2,1,0:T(8,128)}, f32[32,256,256]{2,1,0:T(8,128)}) fusion(f32[32,256,256]{2,1,0:T(8,128)} %get-tuple-element.227, pred[32]{0:T(512)(128)(4,1)S(1)} %compare_bitcast_fusion.2, f32[32,256,256]{2,1,0:T(8,128)} %get-tuple-element.225, f32[32,256,256]{2,1,0:T(8,128)} %get-tuple-element.226), kind=kLoop, calls=%fused_computation.16 | loop fusion | flops 8388608 | bytes 41943072 | tf_op jit(solution)/shard_map/while/body/eval_jaxpr/cond/branch_1_fun/add | solution.py:84
  351.4 15.6 %conditional.15 = ((f32[32,256,256]{2,1,0:T(8,128)}, f32[32,256,256]{2,1,0:T(8,128)})) conditional(s32[]{:T(128)} %convert_element_type.50, (f32[32,256,256]{2,1,0:T(8,128)}, f32[32,256,256]{2,1,0:T(8,128)}) %get-tuple-element.527, (f32[32,256,256]{2,1,0:T(8,128)}, f32[32,256,256]{2,1,0:T(8,128)}, s32[1,32]{1,0:T(1,128)S(1)}, ...), branch_computations={%region_9.9_spmd, %region_10.10_spmd} | conditional | flops 8388640 | bytes 41943256 | solution.py:92
  351.4 15.6 %select_add_fusion.3 = (f32[32,256,256]{2,1,0:T(8,128)}, f32[32,256,256]{2,1,0:T(8,128)}) fusion(f32[32,256,256]{2,1,0:T(8,128)} %get-tuple-element.231, pred[32]{0:T(512)(128)(4,1)S(1)} %compare_bitcast_fusion.3, f32[32,256,256]{2,1,0:T(8,128)} %get-tuple-element.229, f32[32,256,256]{2,1,0:T(8,128)} %get-tuple-element.230), kind=kLoop, calls=%fused_computation.18 | loop fusion | flops 8388608 | bytes 41943072 | tf_op jit(solution)/shard_map/while/body/eval_jaxpr/cond/branch_1_fun/add | solution.py:84
  408.7 15.6 %conditional.13 = ((f32[32,256,256]{2,1,0:T(8,128)}, f32[32,256,256]{2,1,0:T(8,128)})) conditional(s32[]{:T(128)} %convert_element_type.52, (f32[32,256,256]{2,1,0:T(8,128)}, f32[32,256,256]{2,1,0:T(8,128)}) %conditional.12, (f32[32,256,256]{2,1,0:T(8,128)}, f32[32,256,256]{2,1,0:T(8,128)}, s32[1,32]{1,0:T(1,128)S(1)}, ...), branch_computations={%region_5.5_spmd, %region_6.6_spmd} | conditional | flops 8388640 | bytes 41943256 | solution.py:92
  425.0 15.6 %conditional.14 = ((f32[32,256,256]{2,1,0:T(8,128)}, f32[32,256,256]{2,1,0:T(8,128)})) conditional(s32[]{:T(128)} %convert_element_type.51, (f32[32,256,256]{2,1,0:T(8,128)}, f32[32,256,256]{2,1,0:T(8,128)}) %get-tuple-element.526, (f32[32,256,256]{2,1,0:T(8,128)}, f32[32,256,256]{2,1,0:T(8,128)}, s32[1,32]{1,0:T(1,128)S(1)}, ...), branch_computations={%region_7.7_spmd, %region_8.8_spmd} | conditional | flops 8388640 | bytes 41943256 | solution.py:92
  441.2 15.6 %conditional.15 = ((f32[32,256,256]{2,1,0:T(8,128)}, f32[32,256,256]{2,1,0:T(8,128)})) conditional(s32[]{:T(128)} %convert_element_type.50, (f32[32,256,256]{2,1,0:T(8,128)}, f32[32,256,256]{2,1,0:T(8,128)}) %get-tuple-element.527, (f32[32,256,256]{2,1,0:T(8,128)}, f32[32,256,256]{2,1,0:T(8,128)}, s32[1,32]{1,0:T(1,128)S(1)}, ...), branch_computations={%region_9.9_spmd, %region_10.10_spmd} | conditional | flops 8388640 | bytes 41943256 | solution.py:92
  457.4 15.6 %conditional.16 = ((f32[32,256,256]{2,1,0:T(8,128)}, f32[32,256,256]{2,1,0:T(8,128)})) conditional(s32[]{:T(128)} %convert_element_type.49, (f32[32,256,256]{2,1,0:T(8,128)}, f32[32,256,256]{2,1,0:T(8,128)}) %get-tuple-element.528, (f32[32,256,256]{2,1,0:T(8,128)}, f32[32,256,256]{2,1,0:T(8,128)}, s32[1,32]{1,0:T(1,128)S(1)}, ...), branch_computations={%region_11.11_spmd.clone, %region_12.12_spmd.clone} | conditional | flops 8388640 | bytes 41943256 | solution.py:92
  522.6 22.2 %reduce-scatter.5.cloned.1.call-done = f32[32,168]{1,0:T(8,128)} async-done(((f32[128,168]{1,0:T(8,128)}), f32[32,168]{1,0:T(8,128)}) %reduce-scatter.5.cloned.1.call-update) | async-done | bytes 21520 | tf_op jit(solution)/shard_map/reduce_scatter | solution.py:47
  544.8 28.8 %reduce-scatter.11.cloned.1.call-done = f32[16,176]{1,0:T(8,128)} async-done(((f32[64,176]{1,0:T(8,128)}), f32[16,176]{1,0:T(8,128)}) %reduce-scatter.11.cloned.1.call-update) | async-done | bytes 11280 | tf_op jit(solution)/shard_map/reduce_scatter | solution.py:47
  573.6 45.0 %all-reduce.5 = (f32[16,176]{1,0:T(8,128)S(1)}, f32[32,168]{1,0:T(8,128)S(1)}) all-reduce(f32[16,176]{1,0:T(8,128)} %reduce-scatter.11.cloned.1.call-done, f32[32,168]{1,0:T(8,128)} %reduce-scatter.5.cloned.1.call-done), channel_id=11, replica_groups=mesh['frag'=2,'gx_0'=4,'gx_1'=16,'gx_2'=2] {'gx_1'}, use_global_device_ids=true, to_apply=%region_25.26.clone | all-reduce | flops 8192 | bytes 65536
  618.7 17.0 %reduce-scatter.7.cloned.1.call-done = f32[8,168]{1,0:T(8,128)} async-done(((f32[128,168]{1,0:T(8,128)}), f32[8,168]{1,0:T(8,128)}) %reduce-scatter.7.cloned.1.call-update) | async-done | bytes 5392 | tf_op jit(solution)/shard_map/reduce_scatter | solution.py:47
  635.6 16.1 %all-reduce.6 = (f32[8,168]{1,0:T(8,128)S(1)}, f32[2,168]{1,0:T(2,128)S(1)}) all-reduce(f32[8,168]{1,0:T(8,128)} %reduce-scatter.7.cloned.1.call-done, f32[2,168]{1,0:T(2,128)S(1)} %constant_dynamic-slice_fusion.8), channel_id=7, replica_groups=mesh['frag'=2,'gx_0'=4,'gx_1'=16,'gx_2'=2] {'gx_2'}, use_global_device_ids=true, to_apply=%region_21.22.clone | all-reduce | flops 1680 | bytes 13440
  (209 shorter events, 346.8 us)
Async XLA Ops:
  6.5 50.6 %copy-start = (s32[256]{0:T(256)S(1)}, s32[256]{0:T(256)}, u32[]{:S(2)}) copy-start(s32[256]{0:T(256)} %param.26) | copy-start | bytes 3076
  6.6 152.6 %all-gather.3.cloned.1.call-start = ((), (), s32[]{:S(2)}) async-start(), calls=%async_computation.9 | async-start | bytes 1585152 | tf_op jit(solution)/shard_map/all_gather | solution.py:22
  10.1 42.3 %all-to-all-start = ((s32[2,1,128]{0,1,2:T(1,128)}), s32[2,1,128]{0,1,2:T(1,128)S(1)}, u32[]{:S(2)}, u32[]{:S(2)}) async-start(s32[2,1,128]{0,1,2:T(1,128)} %bitcast.15), calls=%async_computation | async-start | bytes 131072 | tf_op jit(solution)/shard_map/all_to_all | solution.py:114
  41.5 476.9 %reduce-scatter.9.cloned.1.call-start = ((), (), s32[]{:S(2)}) async-start(), calls=%async_computation.7 | async-start | bytes 196608 | tf_op jit(solution)/shard_map/reduce_scatter | solution.py:47
  162.2 357.2 %copy-start.5 = (u32[256]{0:T(256)S(1)}, u32[256]{0:T(256)}, u32[]{:S(2)}) copy-start(u32[256]{0:T(256)} %constant.118) | copy-start | bytes 3076
  162.3 357.8 %copy-start.4 = (u32[256]{0:T(256)S(1)}, u32[256]{0:T(256)}, u32[]{:S(2)}) copy-start(u32[256]{0:T(256)} %constant.122) | copy-start | bytes 3076
  162.3 358.4 %copy-start.3 = (u32[256]{0:T(256)S(1)}, u32[256]{0:T(256)}, u32[]{:S(2)}) copy-start(u32[256]{0:T(256)} %constant.130) | copy-start | bytes 3076
  162.3 497.3 %copy-start.2 = (f32[512]{0:T(512)S(1)}, f32[512]{0:T(512)}, u32[]{:S(2)}) copy-start(f32[512]{0:T(512)} %param.25) | copy-start | bytes 6148
  173.8 8.4 %copy-start.1 = (f32[32,256,256]{2,1,0:T(8,128)S(1)}, f32[32,256,256]{2,1,0:T(8,128)}, u32[]{:S(2)}) copy-start(f32[32,256,256]{2,1,0:T(8,128)} %get-tuple-element.463) | copy-start | bytes 25165828 | tf_op jit(solution)/shard_map/while/body/eval_jaxpr/cond
  232.4 8.4 %copy-start.1 = (f32[32,256,256]{2,1,0:T(8,128)S(1)}, f32[32,256,256]{2,1,0:T(8,128)}, u32[]{:S(2)}) copy-start(f32[32,256,256]{2,1,0:T(8,128)} %get-tuple-element.463) | copy-start | bytes 25165828 | tf_op jit(solution)/shard_map/while/body/eval_jaxpr/cond
  306.6 8.4 %copy-start.1 = (f32[32,256,256]{2,1,0:T(8,128)S(1)}, f32[32,256,256]{2,1,0:T(8,128)}, u32[]{:S(2)}) copy-start(f32[32,256,256]{2,1,0:T(8,128)} %get-tuple-element.463) | copy-start | bytes 25165828 | tf_op jit(solution)/shard_map/while/body/eval_jaxpr/cond
  396.4 8.4 %copy-start.1 = (f32[32,256,256]{2,1,0:T(8,128)S(1)}, f32[32,256,256]{2,1,0:T(8,128)}, u32[]{:S(2)}) copy-start(f32[32,256,256]{2,1,0:T(8,128)} %get-tuple-element.463) | copy-start | bytes 25165828 | tf_op jit(solution)/shard_map/while/body/eval_jaxpr/cond
  504.4 40.4 %reduce-scatter.5.cloned.1.call-start = ((), (), s32[]{:S(2)}) async-start(), calls=%async_computation.5 | async-start | bytes 163840 | tf_op jit(solution)/shard_map/reduce_scatter | solution.py:47
  505.2 68.4 %reduce-scatter.11.cloned.1.call-start = ((), (), s32[]{:S(2)}) async-start(), calls=%async_computation.8 | async-start | bytes 81920 | tf_op jit(solution)/shard_map/reduce_scatter | solution.py:47
  518.5 117.2 %reduce-scatter.7.cloned.1.call-start = ((), (), s32[]{:S(2)}) async-start(), calls=%async_computation.6 | async-start | bytes 139264 | tf_op jit(solution)/shard_map/reduce_scatter | solution.py:47
Sparse Core Ops, SparseCore 0:
  9.9 149.2 all-gather.2
  504.5 13.8 reduce-scatter.8
  520.9 23.8 reduce-scatter.4
  547.2 26.4 reduce-scatter.10
  576.0 59.5 reduce-scatter.6
where the time goes:
time: 672 us; the launch traced here: 667 us
  other arithmetic  242 us (36%)
  waiting for transfers between devices  187 us (28%)
  blocking collectives  66.9 us (10%)
  matrix products  56.5 us (8%)
  local copies, waits for them, and re-layouts  51.6 us (8%)
  starting transfers between devices  31.7 us (5%)
  loops' own time  16.2 us (2%)
  between operations  14.7 us (2%)
    add x11, other arithmetic, add_power(): sum_now + jnp.where(power <= angular[:, None, None], term_now / float(2 *...  169 us
    all_gather x1, waiting for transfers between devices, gather_packed(): lines, at, outs = (lax.all_gather(vector, axis), 0, [])  94.6 us
    reduce_scatter x4, waiting for transfers between devices, sum_in_order(): blocks = lax.psum_scatter(blocks, axes[k], scatter_dimension=0, tiled=True)  81.1 us
    unnamed x3, blocking collectives  66.9 us
    dot_general x4, matrix products, tile_terms(): jnp.einsum('tij,tj->ti', kernel, weight_blocks[ket_ids], precision=lax.Pr...  56.5 us
    broadcast_in_dim x4, other arithmetic, add_power(): sum_now + jnp.where(power <= angular[:, None, None], term_now / float(2 *...  33.7 us
    all_to_all x1, starting transfers between devices, shards(): lax.all_to_all(spread, GX, split_axis=2, concat_axis=1, tiled=True)  31.4 us
    div x4, other arithmetic, tile_terms(): ratio = distance / denominator  28.7 us
  transfers between devices with their start and end apart: 6, of which 6 were waited for; matrix products, arithmetic and copies ran while one was open for 3% of the time, Pallas kernels for 0%

commit v1 on v0

v1 whole, which is shorter than its diff:
```python
import functools
from fractions import Fraction
from math import comb

import jax
import jax.numpy as jnp
from jax import lax
from jax.experimental import pallas as pl
from jax.experimental.pallas import tpu as pltpu
from jax.sharding import Mesh
from jax.sharding import PartitionSpec as P

PB = 256
MAXL = 3
NX, NZ, NC = 4, 16, 2
NCHIP = NX * NZ
NDEV = NCHIP * NC
NBLK = 2 * NDEV
GX = ("gx_0", "gx_1", "gx_2")
FRAG_GX = ("frag", "gx_0", "gx_1", "gx_2")
ROWS = 24
BRA_ROW, KET_ROW = 20, 21
MESH = pl.DeviceIdType.MESH
F32, BF16 = jnp.float32, jnp.bfloat16
IO = lambda shape, dim: lax.broadcasted_iota(jnp.int32, shape, dim)


def series_coefficients(kind):
    c = [sum(Fraction((-1) ** n * comb(m, n), 2 * m + 1) for m in range(n, kind + 1)) for n in range(kind + 1)]
    lead = c[kind]
    return float(lead), [float(x / lead) for x in reversed(c[:kind])]


def gather_kernel(coef, expo, cent, dens, tiles, out, chunk, ssem, csem, crecv, zsem, xsem):
    x, z, c = (lax.axis_index(a) for a in GX)
    slot = lambda xx, zz, cc=c: cc * NCHIP + xx * NZ + zz
    zat = lambda d: lax.rem(z + d + NZ, NZ)
    xat = lambda d: lax.rem(x + d + NX, NX)
    own = slot(x, z)

    for r in range(4):
        cut = pl.ds(128 * r, 128)
        for a in range(3):
            chunk[4 * a + r, :] = cent[a, cut]
        chunk[12 + r, :] = expo[cut]
        chunk[16 + r, :] = coef[cut] * dens[cut]
    chunk[BRA_ROW : BRA_ROW + 2, :] = tiles[...].astype(F32)
    chunk[22:24, :] = jnp.zeros((2, 128), F32)
    out[own] = chunk[...]

    barrier = pltpu.get_barrier_semaphore()
    zpeers = [1, -1, 2, -2]
    for d in zpeers:
        pl.semaphore_signal(barrier, inc=1, device_id={"gx_1": zat(d)}, device_id_type=MESH)
    for d in (1, -1):
        pl.semaphore_signal(barrier, inc=1, device_id={"gx_0": xat(d)}, device_id_type=MESH)
    pl.semaphore_signal(barrier, inc=1, device_id={"gx_2": 1 - c}, device_id_type=MESH)
    pl.semaphore_wait(barrier, 7)

    def send(src, at, sem, axis, to):
        pltpu.make_async_remote_copy(
            src_ref=src, dst_ref=out.at[at], send_sem=ssem if axis != "gx_2" else csem, recv_sem=sem,
            device_id={axis: to}, device_id_type=MESH,
        ).start()

    def arrived(at, sem):
        pltpu.make_async_remote_copy(
            src_ref=out.at[at], dst_ref=out.at[at], send_sem=ssem, recv_sem=sem,
            device_id={"gx_2": 1 - c}, device_id_type=MESH,
        ).wait_recv()

    def z_send(src, origin, reach):
        for step in (1, 2):
            d = reach + step * (1 if origin > 0 else -1)
            if -7 <= d <= 8:
                send(src, slot(x, zat(-reach)), zsem.at[d + 7], "gx_1", zat(d - reach))

    def x_send(src, zd):
        at = slot(x, zat(-zd))
        send(src, at, xsem.at[zd + 7, 0], "gx_0", xat(1))
        send(src, at, xsem.at[zd + 7, 1], "gx_0", xat(-1))

    def c_send(src, at):
        send(src, at, crecv, "gx_2", 1 - c)

    def x_take(zd):
        up = slot(xat(-1), zat(-zd))
        down = slot(xat(1), zat(-zd))
        arrived(up, xsem.at[zd + 7, 0])
        if zd % 2 == 0:
            send(out.at[up], up, xsem.at[zd + 7, 2], "gx_0", xat(1))
        c_send(out.at[up], up)
        arrived(down, xsem.at[zd + 7, 1])
        if zd % 2 == 1:
            send(out.at[down], down, xsem.at[zd + 7, 2], "gx_0", xat(-1))
        c_send(out.at[down], down)

    def x_far(zd):
        at = slot(xat(2), zat(-zd))
        arrived(at, xsem.at[zd + 7, 2])
        c_send(out.at[at], at)

    z_send(chunk, 1, 0)
    z_send(chunk, -1, 0)
    x_send(chunk, 0)
    c_send(chunk, own)
    near, far = [0], []
    for rnd in range(1, 5):
        fresh = []
        for d in (2 * rnd, -2 * rnd, 2 * rnd - 1, 1 - 2 * rnd):
            if d < -7:
                continue
            at = slot(x, zat(-d))
            arrived(at, zsem.at[d + 7])
            if d % 2 == 0:
                z_send(out.at[at], d, d)
            x_send(out.at[at], d)
            c_send(out.at[at], at)
            fresh.append(d)
        for d in near:
            x_take(d)
        for d in far:
            x_far(d)
        near, far = fresh, near
    for d in near:
        x_take(d)
    for d in far + near:
        x_far(d)

    plane = out.at[pl.ds((1 - c) * NCHIP, NCHIP)]
    pltpu.make_async_remote_copy(
        src_ref=plane, dst_ref=plane, send_sem=csem, recv_sem=crecv,
        device_id={"gx_2": 1 - c}, device_id_type=MESH,
    ).wait()
    most = out.at[pl.ds(0, NCHIP - 1)]
    pltpu.make_async_remote_copy(
        src_ref=most, dst_ref=most, send_sem=ssem, recv_sem=crecv,
        device_id={"gx_2": 1 - c}, device_id_type=MESH,
    ).wait_send()


def gather_all(coefficient, exponent, centers, density, tile_list):
    return pl.pallas_call(
        gather_kernel,
        out_shape=jax.ShapeDtypeStruct((NDEV, ROWS, 128), F32),
        in_specs=[pl.BlockSpec(memory_space=pltpu.VMEM)] * 5,
        out_specs=pl.BlockSpec(memory_space=pltpu.VMEM),
        scratch_shapes=[
            pltpu.VMEM((ROWS, 128), F32),
            pltpu.SemaphoreType.DMA,
            pltpu.SemaphoreType.DMA,
            pltpu.SemaphoreType.DMA,
            pltpu.SemaphoreType.DMA((16,)),
            pltpu.SemaphoreType.DMA((16, 3)),
        ],
        compiler_params=pltpu.CompilerParams(collective_id=0, has_side_effects=True),
        name="gather_pairs",
    )(coefficient, exponent, centers, density, tile_list)


def split3(v):
    h = v.astype(BF16).astype(F32)
    m = (v - h).astype(BF16).astype(F32)
    return h, m, v - h - m


def ket_rows(v):
    h, m, l = split3(v)
    return jnp.concatenate([h, m, l, h, m, h], axis=0)


def bra_rows(v):
    h, m, l = split3(v)
    return jnp.concatenate([h, h, h, m, m, l], axis=0)


def dot(a, b, dims=((1,), (0,)), **kw):
    return lax.dot_general(a, b, (dims, ((), ())), preferred_element_type=F32, **kw)


NTDIMS = ((1,), (1,))


def tile_kernel(me, ang_s, ang_v, g, coef, core, out, table, feat, ebc, acc, den, lists, slist, sem):
    if me is None:
        x, z, c = (lax.axis_index(a) for a in GX)
        me = (x * NZ + z) * NC + c

    def relayout(p, carry):
        d = lax.rem(p, NCHIP) * NC + p // NCHIP
        base = pl.multiple_of(d * 32, 32)
        cx, cy, cz, e, w = (g[p, 4 * v : 4 * v + 4, :] for v in range(5))
        n = cx * cx + cy * cy + cz * cz + e
        for v, val in enumerate((-2.0 * cx, -2.0 * cy, -2.0 * cz, n, jnp.ones_like(n), e, w, jnp.zeros_like(n))):
            table[pl.ds(base + v, 4, stride=8), :] = val
        return carry

    lax.fori_loop(0, NDEV, relayout, 0, unroll=4)

    bra = g[:, BRA_ROW, :].astype(jnp.int32) - 2 * me
    ket = g[:, KET_ROW, :].astype(jnp.int32)
    mine = (bra >= 0) & (bra < 2)
    high = jnp.where(mine, bra * 16 + ket // 16, -1)
    low = ket & 15
    count = jnp.zeros((32, 16), F32)
    step = 16
    for r in range(0, NDEV, step):
        a = [(IO((32, 128), 0) == high[r + k : r + k + 1, :]).astype(F32).astype(BF16) for k in range(step)]
        b = [(IO((16, 128), 0) == low[r + k : r + k + 1, :]).astype(F32).astype(BF16) for k in range(step)]
        count = count + dot(jnp.concatenate(a, axis=1), jnp.concatenate(b, axis=1), NTDIMS)
    spread = (IO((16, 256), 1) % 16 == IO((16, 256), 0)).astype(F32)
    wide = dot(count, spread, precision=lax.Precision.HIGHEST)
    wide = jnp.where(IO((32, 256), 0) % 16 == IO((32, 256), 1) // 16, wide, 0.0)
    mult = [jnp.sum(wide[16 * b : 16 * b + 16], axis=0, keepdims=True) for b in range(2)]

    ang_row = ang_v[...].reshape(1, NBLK)
    row_i, col_i = IO((NBLK, NBLK), 0), IO((NBLK, NBLK), 1)
    key_row = ang_row * NBLK + IO((1, NBLK), 1)
    key_col = jnp.sum(jnp.where(row_i == col_i, key_row.astype(F32), 0.0), axis=1, keepdims=True).astype(jnp.int32)
    before = (key_col < key_row).astype(F32).astype(BF16)
    level = (key_col < IO((NBLK, 128), 1) * NBLK).astype(F32).astype(BF16)
    valid = [(m > 0.0).astype(F32) for m in mult]
    valid8 = jnp.concatenate(valid + [jnp.zeros((6, NBLK), F32)], axis=0).astype(BF16)
    rank = dot(valid8, before)
    starts = dot(valid8, level)
    ids = IO((1, NBLK), 1).astype(F32)
    for b in range(2):
        where_b = jnp.where(valid[b] > 0.0, rank[b : b + 1].astype(jnp.int32), -1)
        onehot = (where_b == row_i).astype(F32).astype(BF16)
        m_hi = jnp.floor(mult[b] * (1.0 / 16.0))
        src = jnp.concatenate([ids, mult[b] - 16.0 * m_hi, m_hi, jnp.zeros((5, NBLK), F32)], axis=0).astype(BF16)
        got = dot(src, onehot, NTDIMS)
        lists[2 * b : 2 * b + 1, :] = got[0:1].astype(jnp.int32)
        lists[2 * b + 1 : 2 * b + 2, :] = (got[1:2] + 16.0 * got[2:3]).astype(jnp.int32)
        lists[4 + b : 5 + b, 0:128] = starts[b : b + 1].astype(jnp.int32)
    to_smem = pltpu.make_async_copy(lists, slist, sem)
    to_smem.start()

    for q in range(4):
        grp = table[pl.ds(pl.multiple_of(me * 32 + 8 * q, 8), 8), :]
        v = grp[0:3] * -0.5
        v = jnp.concatenate([v, jnp.ones((1, 128), F32), grp[3:4], jnp.zeros((3, 128), F32)], axis=0)
        full = jnp.concatenate([bra_rows(v), grp, jnp.zeros((72, 128), F32)], axis=0).T
        feat[128 * q : 128 * q + 128, :] = full[:, 0:48].astype(BF16)
        ebc[128 * q : 128 * q + 128, :] = jnp.broadcast_to(full[:, 53:54], (128, 128))
    acc[...] = jnp.zeros_like(acc)
    to_smem.wait()

    CH = 64

    def ket_side(b, p):
        k = slist[2 * b, p]
        rows = [table[pl.ds(pl.multiple_of(k * 16 + 8 * h, 8), 8), :] for h in range(2)]
        return jnp.concatenate([ket_rows(v) for v in rows], axis=1).astype(BF16)

    for b in range(2):
        total = slist[4 + b, 4]

        @pl.when(total > 0)
        def _():
            rhs = ket_side(b, 0)
            den[0] = dot(feat[256 * b : 256 * b + 256, :], rhs)

            def run(kind, lo, hi):
                lead, lower = series_coefficients(kind)

                def body(p, carry):
                    now = lax.rem(p, 2)
                    rhs = ket_side(b, jnp.minimum(p + 1, NBLK - 1))
                    k = slist[2 * b, p]
                    times = slist[2 * b + 1, p].astype(F32) * lead
                    er, wr = [], []
                    for h in range(2):
                        at = k * 16 + 8 * h
                        er.append(jnp.broadcast_to(table[pl.ds(at + 5, 1), :], (8, 128)))
                        wr.append(jnp.broadcast_to(table[pl.ds(at + 6, 1), :] * times, (8, 128)))
                    for i in range(0, PB, CH):
                        cut = pl.ds(256 * b + i, CH)
                        nxt = dot(feat[cut, :], rhs)
                        sums = None
                        for h in range(2):
                            d = den[now, i : i + CH, 128 * h : 128 * h + 128].reshape(CH // 8, 8, 128)
                            r = lax.rsqrt(d)
                            v = r * wr[h]
                            if kind:
                                t = (ebc[cut, :].reshape(CH // 8, 8, 128) + er[h]) * (r * r)
                                poly = t + lower[0]
                                for coefficient in lower[1:]:
                                    poly = poly * t + coefficient
                                v = v * poly
                            sums = v if sums is None else sums + v
                        acc[cut, :] += sums.reshape(CH, 128)
                        den[1 - now, i : i + CH, :] = nxt
                    return carry

                lax.fori_loop(lo, hi, body, 0)

            ang_b = ang_s[2 * me + b]
            for l in range(MAXL + 1):
                lo, hi = slist[4 + b, l], slist[4 + b, l + 1]
                lax.switch(ang_b + l - l, [functools.partial(run, a + l, lo, hi) for a in range(MAXL + 1)])

    for q in range(4):
        total = jnp.sum(acc[128 * q : 128 * q + 128, :].T, axis=0)
        cut = pl.ds(128 * q, 128)
        out[cut] = core[cut] + coef[cut] * total


def tile_sums(gathered, shell_ang, coefficient, core_fock, me=None, interpret=False):
    vm = pl.BlockSpec(memory_space=pltpu.VMEM)
    return pl.pallas_call(
        functools.partial(tile_kernel, me),
        out_shape=jax.ShapeDtypeStruct((2 * PB,), F32),
        in_specs=[pl.BlockSpec(memory_space=pltpu.SMEM), vm, vm, vm, vm],
        out_specs=vm,
        scratch_shapes=[
            pltpu.VMEM((NBLK * 16, 128), F32),
            pltpu.VMEM((2 * PB, 48), BF16),
            pltpu.VMEM((2 * PB, 128), F32),
            pltpu.VMEM((2 * PB, 128), F32),
            pltpu.VMEM((2, PB, PB), F32),
            pltpu.VMEM((8, NBLK), jnp.int32),
            pltpu.SMEM((8, NBLK), jnp.int32),
            pltpu.SemaphoreType.DMA,
        ],
        name="tile_sums",
        interpret=interpret,
    )(shell_ang, shell_ang, gathered, coefficient, core_fock)


def shards(coefficient, exponent, centers, density, core_fock, shell_ang, tile_list):
    gathered = gather_all(coefficient, exponent, centers, density, tile_list)
    return tile_sums(gathered, shell_ang, coefficient, core_fock)


def solution(mesh):
    finer = Mesh(mesh.devices.reshape(mesh.shape["frag"], NX, NZ, NC), FRAG_GX)
    return jax.shard_map(
        shards,
        mesh=finer,
        in_specs=(
            P(FRAG_GX),
            P(FRAG_GX),
            P(None, FRAG_GX),
            P(FRAG_GX),
            P(FRAG_GX),
            P("frag"),
            P(None, FRAG_GX),
        ),
        out_specs=P(FRAG_GX),
        check_vma=False,
    )
```

time: 672 us -> 79.5 us (0.12)
  other arithmetic: 242 us -> 0 us
  waiting for transfers between devices: 187 us -> 0 us
  Pallas kernels: 0 us -> 79.5 us
  blocking collectives: 66.9 us -> 0 us
  matrix products: 56.5 us -> 0 us
  local copies, waits for them, and re-layouts: 51.6 us -> 0 us
  starting transfers between devices: 31.7 us -> 0 us
  loops' own time: 16.2 us -> 0 us
  between operations: 14.7 us -> 0.01 us
    add x13 -> x0, other arithmetic: 169 us -> none  [the longest x11 169 us: add_power(): sum_now + jnp.where(power <= angular[:, None, None], term_now / float(2 *...]
    all_gather x1 -> x0, waiting for transfers between devices: 94.6 us -> none  [gather_packed(): lines, at, outs = (lax.all_gather(vector, axis), 0, [])]
    reduce_scatter x4 -> x0, waiting for transfers between devices: 81.1 us -> none  [sum_in_order(): blocks = lax.psum_scatter(blocks, axes[k], scatter_dimension=0, tiled=True)]
    pallas_call x0 -> x2, Pallas kernels: none -> 79.5 us  [the longest x1 45.3 us: gather_all(): pl.pallas_call(gather_kernel, out_shape=jax.ShapeDtypeStruct((NDEV, ROWS,...]
    unnamed x3 -> x0, blocking collectives: 66.9 us -> none
    dot_general x4 -> x0, matrix products: 56.5 us -> none  [tile_terms(): jnp.einsum('tij,tj->ti', kernel, weight_blocks[ket_ids], precision=lax.Pr...]
    broadcast_in_dim x4 -> x0, other arithmetic: 33.7 us -> none  [add_power(): sum_now + jnp.where(power <= angular[:, None, None], term_now / float(2 *...]
    all_to_all x1 -> x0, starting transfers between devices: 31.4 us -> none  [shards(): lax.all_to_all(spread, GX, split_axis=2, concat_axis=1, tiled=True)]
  transfers between devices with their start and end apart: 6 -> 0, of which waited for: 6 -> 0; matrix products, arithmetic and copies ran while one was open for 3% -> 0% of each run, Pallas kernels for 0% -> 0%
where the time goes in v1:
time: 79.5 us; the launch traced here: 79.6 us
  Pallas kernels  79.5 us (100%)
    pallas_call x1, Pallas kernels, gather_all(): pl.pallas_call(gather_kernel, out_shape=jax.ShapeDtypeStruct((NDEV, ROWS,...  45.3 us
    pallas_call x1, Pallas kernels, tile_sums(): pl.pallas_call(functools.partial(tile_kernel, me), out_shape=jax.ShapeDty...  34.2 us

profile of v1, /device:TPU:47, one launch (start us, length us, event | category | flops | bytes accessed | tf_op | source)
XLA Modules:
  0.0 79.6 jit_solution(7907555386400847003)
XLA Ops:
  0.0 45.3 %gather_pairs.1.g = f32[128,24,128]{2,1,0:T(8,128)} custom-call(f32[512]{0:T(512)} %coef.3, f32[512]{0:T(512)} %expo.1, f32[3,512]{1,0:T(4,128)} %cent.1, f32[512]{0:T(512)} %dens.1, s32[2,128]{1,0:T(2,128)} %tiles.1), custom_call_target="tpu_custom_call" | custom-call | tf_op jit(solution)/shard_map/gather_pairs/pallas_call | solution.py:143
  45.3 34.2 %tile_sums.1 = f32[512]{0:T(512)} custom-call(s32[256]{0:T(256)} %ang_v.1, s32[256]{0:T(256)} %ang_v.1, f32[128,24,128]{2,1,0:T(8,128)} %gather_pairs.1.g, f32[512]{0:T(512)} %coef.3, f32[512]{0:T(512)} %core.1), custom_call_target="tpu_custom_call" | custom-call | tf_op jit(solution)/shard_map/tile_sums/pallas_call | solution.py:311
